TPU v7x, 32 devices: a whole 2x2x4 slice. The times are simulated.
32 devices in a mesh: face: 8 (over z, y), col: 4 (over x, core).
Axes of the slice: x: 2, y: 2, z: 4, core: 2. Of those that a mesh axis runs over, the one named last changes fastest.
Arguments:
- fields: float32 [4, 160, 80, 128], P(None, 'face', 'col'), may hold values from -6 to 6
- metric_diag: float32 [2, 160, 80], P(None, 'face', 'col'), may hold values from 0.05 to 0.5
- metric_cross: float32 [160, 80], P('face', 'col'), may hold values from -0.1 to 0.1
- point_mass: float32 [160, 80], P('face', 'col'), may hold values from 0.5 to 2
Outputs:
- biharmonic: float32 [4, 160, 80, 128], P(None, 'face', 'col')
All inputs are finite; a program needn't handle non-finite values.
Results may differ from a plain program's by a relative error of at most 0.00024.
Values sent between devices are 32-bit elements; how exact they have to be, the bound alone decides.
A program may use at most 64 MiB of HBM per device.

v0:
```python
import jax
import jax.numpy as jnp
import numpy as np
from jax import lax
from jax.sharding import PartitionSpec as P


def with_halo(array, sides, width):
    for axis, dim in sides:
        devices, length = (lax.axis_size(axis), array.shape[dim])
        up = [(i, (i + 1) % devices) for i in range(devices)]
        down = [(j, i) for i, j in up]
        last = lax.slice_in_dim(array, length - width, length, axis=dim)
        first = lax.slice_in_dim(array, 0, width, axis=dim)
        before = lax.ppermute(last, axis, up)
        after = lax.ppermute(first, axis, down)
        array = jnp.concatenate([before, array, after], axis=dim)
    return array


def derivative_table():
    small = 1.0 / np.sqrt(5.0)
    nodes = np.array([-1.0, -small, small, 1.0])
    count = nodes.shape[0]
    weights = np.array(
        [np.prod([nodes[a] - nodes[k] for k in range(count) if k != a]) for a in range(count)]
    )
    table = np.zeros((count, count))
    for a in range(count):
        for b in range(count):
            if a == b:
                table[a, b] = np.sum([1.0 / (nodes[a] - nodes[k]) for k in range(count) if k != a])
            else:
                table[a, b] = weights[a] / weights[b] / (nodes[a] - nodes[b])
    return jnp.asarray(table, jnp.float32)


def laplace(values, metric_diag, metric_cross):
    table = derivative_table()
    nfield, rows, cols, nlev = values.shape
    blocks_x = rows // 4
    blocks_y = cols // 4
    shaped = values.reshape(nfield, blocks_x, 4, blocks_y, 4, nlev)
    first_diag = metric_diag[0].reshape(1, blocks_x, 4, blocks_y, 4, 1)
    second_diag = metric_diag[1].reshape(1, blocks_x, 4, blocks_y, 4, 1)
    cross_term = metric_cross.reshape(1, blocks_x, 4, blocks_y, 4, 1)
    high = lax.Precision.HIGHEST
    grad_x = jnp.einsum("ab,febgcl->feagcl", table, shaped, precision=high)
    grad_y = jnp.einsum("cd,febgdl->febgcl", table, shaped, precision=high)
    flux_x = first_diag * grad_x + cross_term * grad_y
    flux_y = cross_term * grad_x + second_diag * grad_y
    weak = jnp.einsum("ba,febgcl->feagcl", table, flux_x, precision=high)
    weak = weak + jnp.einsum("dc,febgdl->febgcl", table, flux_y, precision=high)
    return (-weak).reshape(nfield, rows, cols, nlev)


def assemble(padded):
    rows = padded.shape[1] - 2
    cols = padded.shape[2] - 2
    row_local = jnp.arange(rows, dtype=jnp.int32) % 4
    col_local = jnp.arange(cols, dtype=jnp.int32) % 4
    row_low = (row_local == 0).astype(jnp.float32).reshape(1, rows, 1, 1)
    row_high = (row_local == 3).astype(jnp.float32).reshape(1, rows, 1, 1)
    col_low = (col_local == 0).astype(jnp.float32).reshape(1, 1, cols, 1)
    col_high = (col_local == 3).astype(jnp.float32).reshape(1, 1, cols, 1)
    summed = padded[:, 1:-1] + row_low * padded[:, :-2] + row_high * padded[:, 2:]
    return summed[:, :, 1:-1] + col_low * summed[:, :, :-2] + col_high * summed[:, :, 2:]


def shards(fields, metric_diag, metric_cross, point_mass):
    local_mass = point_mass[None, :, :, None]
    first_lap = laplace(fields, metric_diag, metric_cross)
    padded_lap, padded_mass = (
        with_halo(first_lap, (("face", 1), ("col", 2)), 1),
        with_halo(local_mass, (("face", 1), ("col", 2)), 1),
    )
    mass_sum = assemble(padded_mass)
    first = assemble(padded_lap) / mass_sum
    second_lap = laplace(first, metric_diag, metric_cross)
    padded_second = with_halo(second_lap, (("face", 1), ("col", 2)), 1)
    return assemble(padded_second) / mass_sum


def solution(mesh):
    return jax.shard_map(
        shards,
        mesh=mesh,
        in_specs=(
            P(None, "face", "col", None),
            P(None, "face", "col"),
            P("face", "col"),
            P("face", "col"),
        ),
        out_specs=P(None, "face", "col", None),
        check_vma=False,
    )
```

profile of v0, /device:TPU:1, one launch (start us, length us, event | category | flops | bytes accessed | tf_op | source)
XLA Modules:
  0.0 51.2 jit_solution(9082121004730212008)
XLA Ops:
  0.0 0.8 %fusion.41 = (f32[1,1,20,1]{2,1,3,0:T(1,128)S(1)}, f32[1,1,20,1]{2,1,3,0:T(1,128)S(1)}) fusion(f32[1,20,20,1]{2,1,3,0:T(8,128)} %bitcast.70), kind=kLoop, calls=%fused_computation.78 | loop fusion | bytes 320 | tf_op jit(solution)/shard_map/slice | solution.py:13
  0.8 2.1 %collective-permute-start.4 = (f32[1,1,20,1]{2,1,3,0:T(1,128)S(1)}, f32[1,1,20,1]{2,1,3,0:T(1,128)S(1)}, u32[]{:S(2)}, u32[]{:S(2)}) collective-permute-start(f32[1,1,20,1]{2,1,3,0:T(1,128)S(1)} %get-tuple-element.17), channel_id=1, source_target_pairs={{0,4},{4,8},{8,12},{12,16},{16,20},{20,24},{24,28},{28,0},{1,5},{5... | collective-permute-start | bytes 248 | tf_op jit(solution)/shard_map/ppermute | solution.py:15
  2.8 3.0 %collective-permute-start.5 = (f32[1,1,20,1]{2,1,3,0:T(1,128)S(1)}, f32[1,1,20,1]{2,1,3,0:T(1,128)S(1)}, u32[]{:S(2)}, u32[]{:S(2)}) collective-permute-start(f32[1,1,20,1]{2,1,3,0:T(1,128)S(1)} %get-tuple-element.18), channel_id=1, source_target_pairs={{4,0},{8,4},{12,8},{16,12},{20,16},{24,20},{28,24},{0,28},{5,1},{9... | collective-permute-start | bytes 248 | tf_op jit(solution)/shard_map/ppermute | solution.py:16
  5.9 0.9 %slice_reduce_fusion.1 = (f32[20,20]{1,0:T(8,128)S(1)}, f32[20,20]{1,0:T(8,128)S(1)}) fusion(f32[2,20,20]{2,0,1:T(2,128)} %param.7), kind=kLoop, calls=%fused_computation.71 | loop fusion | bytes 6400 | tf_op jit(solution)/shard_map/slice | solution.py:44
  8.7 1.5 %fusion.21 = f32[4,4,5,4,5,128]{5,0,4,3,2,1:T(4,128)S(1)} fusion(f32[4,4,1,1,1,1]{1,0,5,4,3,2:T(4,128)S(1)} %copy-done.1, f32[4,5,4,5,4,128]{5,0,4,3,2,1:T(4,128)S(1)} %bitcast.61), kind=kOutput, calls=%fused_computation.41 | convolution fusion | flops 9830400 | bytes 1638464 | tf_op jit(solution)/shard_map/cd,febgdl->febgcl/dot_general | solution.py:49
  10.1 2.0 %bitcast_add_fusion.3 = (f32[4,5,4,5,4,128]{5,2,4,3,1,0:T(4,128)S(1)}, f32[4,5,4,5,4,128]{5,2,4,3,1,0:T(4,128)S(1)}) fusion(f32[4,4,5,4,5,128]{5,0,4,3,2,1:T(4,128)S(1)} %fusion.21, f32[5,4,5,4]{1,3,2,0:T(4,128)S(1)} %copy.33, f32[5,4,5,4]{1,3,2,0:T(4,128)S(1)} %copy.28, f32[4,4,1,1,1,1]{1,0,5,4,3,2:T(4,128)S(1)} %copy-done.1, ...), kind=kOutput, calls=%fused_computation.30 | convolution fusion | flops 10444800 | bytes 3280064 | tf_op jit(solution)/shard_map/ab,febgcl->feagcl/dot_general | solution.py:48
  12.1 1.6 %fusion.19 = f32[4,5,4,5,128,4]{4,5,3,2,1,0:T(4,128)S(1)} fusion(f32[4,4,1,1,1,1]{1,0,5,4,3,2:T(4,128)S(1)} %copy-done.1, f32[4,5,4,5,4,128]{5,2,4,3,1,0:T(4,128)S(1)} %get-tuple-element.19), kind=kOutput, calls=%fused_computation.39 | convolution fusion | flops 9830400 | bytes 1638464 | tf_op jit(solution)/shard_map/dc,febgdl->febgcl/dot_general | solution.py:53
  13.7 1.9 %fusion.1 = f32[4,5,4,5,4,128]{5,2,4,3,1,0:T(4,128)S(1)} fusion(f32[4,4,1,1,1,1]{1,0,5,4,3,2:T(4,128)S(1)} %copy-done.1, f32[4,5,4,5,128,4]{4,5,3,2,1,0:T(4,128)S(1)} %fusion.19, f32[4,5,4,5,4,128]{5,2,4,3,1,0:T(4,128)S(1)} %get-tuple-element.20, f32[4,4,5,4,5,128]{5,0,4,3,2,1:T(4,128)S(1)} %fusion.21, f32[5,4,5,4]{1,3,2,0:T(4,128)S(1)} %copy.28, ...), kind=kOutput, calls=%fused_computation.5 | convolution fusion | flops 10854400 | bytes 3280064 | tf_op jit(solution)/shard_map/ba,febgcl->feagcl/dot_general | solution.py:52
  16.0 4.1 %collective-permute-start.1 = (f32[4,1,20,128]{3,0,2,1:T(4,128)S(1)}, f32[4,1,20,128]{3,0,2,1:T(4,128)S(1)}, u32[]{:S(2)}, u32[]{:S(2)}) collective-permute-start(f32[4,1,20,128]{3,0,2,1:T(4,128)S(1)} %get-tuple-element.14), channel_id=1, source_target_pairs={{4,0},{8,4},{12,8},{16,12},{20,16},{24,20},{28,24},{0,28},{5,1},{9... | collective-permute-start | bytes 122888 | tf_op jit(solution)/shard_map/ppermute | solution.py:16
  20.3 2.8 %collective-permute-start.6 = (f32[1,22,1,1]{2,1,3,0:T(8,128)S(1)}, f32[1,22,1,1]{2,1,3,0:T(8,128)S(1)}, u32[]{:S(2)}, u32[]{:S(2)}) collective-permute-start(f32[1,22,1,1]{2,1,3,0:T(8,128)S(1)} %get-tuple-element.15), channel_id=1, source_target_pairs={{0,1},{1,2},{2,3},{3,0},{4,5},{5,6},{6,7},{7,4},{8,9},{9,10},{10,1... | collective-permute-start | bytes 272 | tf_op jit(solution)/shard_map/ppermute | solution.py:15
  23.1 0.8 %collective-permute-done.6 = f32[1,22,1,1]{2,1,3,0:T(8,128)S(1)} collective-permute-done((f32[1,22,1,1]{2,1,3,0:T(8,128)S(1)}, f32[1,22,1,1]{2,1,3,0:T(8,128)S(1)}, u32[]{:S(2)}, u32[]{:S(2)}) %collective-permute-start.6) | collective-permute-done | bytes 120 | tf_op jit(solution)/shard_map/ppermute | solution.py:15
  23.9 2.3 %collective-permute-done.7 = f32[1,22,1,1]{2,1,3,0:T(8,128)S(1)} collective-permute-done((f32[1,22,1,1]{2,1,3,0:T(8,128)S(1)}, f32[1,22,1,1]{2,1,3,0:T(8,128)S(1)}, u32[]{:S(2)}, u32[]{:S(2)}) %collective-permute-start.7) | collective-permute-done | bytes 120 | tf_op jit(solution)/shard_map/ppermute | solution.py:16
  27.7 2.5 %collective-permute-done.3 = f32[4,22,1,128]{3,0,2,1:T(4,128)S(1)} collective-permute-done((f32[4,22,1,128]{3,0,2,1:T(4,128)S(1)}, f32[4,22,1,128]{3,0,2,1:T(4,128)S(1)}, u32[]{:S(2)}, u32[]{:S(2)}) %collective-permute-start.3) | collective-permute-done | bytes 45088 | tf_op jit(solution)/shard_map/ppermute | solution.py:16
  30.7 0.7 %fusion.12 = f32[4,20,20,128]{3,0,2,1:T(4,128)S(1)} fusion(f32[4,20,22,128]{3,0,2,1:T(4,128)S(1)} %fusion.6, f32[20,20]{1,0:T(8,128)S(1)} %fusion.34, f32[20]{0:T(128)S(1)} %get-tuple-element.23, f32[20]{0:T(128)S(1)} %get-tuple-element.24), kind=kLoop, calls=%fused_computation.25 | loop fusion | flops 1024000 | bytes 3278560 | tf_op jit(solution)/shard_map/div | solution.py:78
  31.5 1.5 %fusion.16 = f32[4,5,4,5,128,4]{4,5,3,2,1,0:T(4,128)S(1)} fusion(f32[4,4,1,1,1,1]{1,0,5,4,3,2:T(4,128)S(1)} %copy-done.1, f32[4,5,4,5,4,128]{5,0,4,3,2,1:T(4,128)S(1)} %bitcast.68), kind=kOutput, calls=%fused_computation.36 | convolution fusion | flops 9830400 | bytes 1638464 | tf_op jit(solution)/shard_map/cd,febgdl->febgcl/dot_general | solution.py:49
  33.0 2.0 %bitcast_add_fusion = (f32[4,5,4,5,4,128]{5,2,4,3,1,0:T(4,128)S(1)}, f32[4,5,4,5,4,128]{5,2,4,3,1,0:T(4,128)S(1)}) fusion(f32[4,5,4,5,128,4]{4,5,3,2,1,0:T(4,128)S(1)} %fusion.16, f32[5,4,5,4]{1,3,2,0:T(4,128)S(1)} %copy.33, f32[5,4,5,4]{1,3,2,0:T(4,128)S(1)} %copy.28, f32[4,4,1,1,1,1]{1,0,5,4,3,2:T(4,128)S(1)} %copy-done.1, ...), kind=kOutput, calls=%fused_computation.28 | convolution fusion | flops 10444800 | bytes 3280064 | tf_op jit(solution)/shard_map/ab,febgcl->feagcl/dot_general | solution.py:48
  35.0 1.6 %fusion.14 = f32[4,5,4,5,128,4]{4,5,3,2,1,0:T(4,128)S(1)} fusion(f32[4,4,1,1,1,1]{1,0,5,4,3,2:T(4,128)S(1)} %copy-done.1, f32[4,5,4,5,4,128]{5,2,4,3,1,0:T(4,128)S(1)} %get-tuple-element.21), kind=kOutput, calls=%fused_computation.34 | convolution fusion | flops 9830400 | bytes 1638464 | tf_op jit(solution)/shard_map/dc,febgdl->febgcl/dot_general | solution.py:53
  36.6 1.9 %fusion.3 = f32[4,5,4,5,4,128]{5,2,4,3,1,0:T(4,128)S(1)} fusion(f32[4,4,1,1,1,1]{1,0,5,4,3,2:T(4,128)S(1)} %copy-done.1, f32[4,5,4,5,128,4]{4,5,3,2,1,0:T(4,128)S(1)} %fusion.14, f32[4,5,4,5,4,128]{5,2,4,3,1,0:T(4,128)S(1)} %get-tuple-element.22, f32[4,5,4,5,128,4]{4,5,3,2,1,0:T(4,128)S(1)} %fusion.16, f32[5,4,5,4]{1,3,2,0:T(4,128)S(1)} %copy.28, ...), kind=kOutput, calls=%fused_computation.7 | convolution fusion | flops 10854400 | bytes 3280064 | tf_op jit(solution)/shard_map/ba,febgcl->feagcl/dot_general | solution.py:52
  38.9 4.1 %collective-permute-start.9 = (f32[4,1,20,128]{3,0,2,1:T(4,128)S(1)}, f32[4,1,20,128]{3,0,2,1:T(4,128)S(1)}, u32[]{:S(2)}, u32[]{:S(2)}) collective-permute-start(f32[4,1,20,128]{3,0,2,1:T(4,128)S(1)} %get-tuple-element.12), channel_id=1, source_target_pairs={{4,0},{8,4},{12,8},{16,12},{20,16},{24,20},{28,24},{0,28},{5,1},{9... | collective-permute-start | bytes 122888 | tf_op jit(solution)/shard_map/ppermute | solution.py:16
  43.1 1.4 %collective-permute-done.8 = f32[4,1,20,128]{3,0,2,1:T(4,128)S(1)} collective-permute-done((f32[4,1,20,128]{3,0,2,1:T(4,128)S(1)}, f32[4,1,20,128]{3,0,2,1:T(4,128)S(1)}, u32[]{:S(2)}, u32[]{:S(2)}) %collective-permute-start.8) | collective-permute-done | bytes 40992 | tf_op jit(solution)/shard_map/ppermute | solution.py:15
  44.5 1.2 %collective-permute-start.10 = (f32[4,22,1,128]{3,0,2,1:T(4,128)S(1)}, f32[4,22,1,128]{3,0,2,1:T(4,128)S(1)}, u32[]{:S(2)}, u32[]{:S(2)}) collective-permute-start(f32[4,22,1,128]{3,0,2,1:T(4,128)S(1)} %get-tuple-element.7), channel_id=1, source_target_pairs={{0,1},{1,2},{2,3},{3,0},{4,5},{5,6},{6,7},{7,4},{8,9},{9,10},{10,1... | collective-permute-start | bytes 135176 | tf_op jit(solution)/shard_map/ppermute | solution.py:15
  45.7 1.1 %collective-permute-done.10 = f32[4,22,1,128]{3,0,2,1:T(4,128)S(1)} collective-permute-done((f32[4,22,1,128]{3,0,2,1:T(4,128)S(1)}, f32[4,22,1,128]{3,0,2,1:T(4,128)S(1)}, u32[]{:S(2)}, u32[]{:S(2)}) %collective-permute-start.10) | collective-permute-done | bytes 45088 | tf_op jit(solution)/shard_map/ppermute | solution.py:15
  46.8 2.3 %collective-permute-done.11 = f32[4,22,1,128]{3,0,2,1:T(4,128)S(1)} collective-permute-done((f32[4,22,1,128]{3,0,2,1:T(4,128)S(1)}, f32[4,22,1,128]{3,0,2,1:T(4,128)S(1)}, u32[]{:S(2)}, u32[]{:S(2)}) %collective-permute-start.11) | collective-permute-done | bytes 45088 | tf_op jit(solution)/shard_map/ppermute | solution.py:16
  49.7 1.5 %fusion.9 = f32[4,20,20,128]{3,0,2,1:T(4,128)} fusion(f32[4,20,22,128]{3,0,2,1:T(4,128)S(1)} %fusion.4, f32[20,20]{1,0:T(8,128)S(1)} %fusion.34, f32[20]{0:T(128)S(1)} %get-tuple-element.23, f32[20]{0:T(128)S(1)} %get-tuple-element.24), kind=kLoop, calls=%fused_computation.20 | loop fusion | flops 1024000 | bytes 3278560 | tf_op jit(solution)/shard_map/div | solution.py:81
  (42 shorter events, 5.3 us)
Async XLA Ops:
  0.0 8.2 %copy-start = (f32[4,20,20,128]{3,0,2,1:T(4,128)S(1)}, f32[4,20,20,128]{3,0,2,1:T(4,128)}, u32[]{:S(2)}) copy-start(f32[4,20,20,128]{3,0,2,1:T(4,128)} %param.6) | copy-start | bytes 2457604
  0.8 19.4 %collective-permute-start.4 = (f32[1,1,20,1]{2,1,3,0:T(1,128)S(1)}, f32[1,1,20,1]{2,1,3,0:T(1,128)S(1)}, u32[]{:S(2)}, u32[]{:S(2)}) collective-permute-start(f32[1,1,20,1]{2,1,3,0:T(1,128)S(1)} %get-tuple-element.17), channel_id=1, source_target_pairs={{0,4},{4,8},{8,12},{12,16},{16,20},{20,24},{24,28},{28,0},{1,5},{5... | collective-permute-start | bytes 248 | tf_op jit(solution)/shard_map/ppermute | solution.py:15
  2.8 17.4 %collective-permute-start.5 = (f32[1,1,20,1]{2,1,3,0:T(1,128)S(1)}, f32[1,1,20,1]{2,1,3,0:T(1,128)S(1)}, u32[]{:S(2)}, u32[]{:S(2)}) collective-permute-start(f32[1,1,20,1]{2,1,3,0:T(1,128)S(1)} %get-tuple-element.18), channel_id=1, source_target_pairs={{4,0},{8,4},{12,8},{16,12},{20,16},{24,20},{28,24},{0,28},{5,1},{9... | collective-permute-start | bytes 248 | tf_op jit(solution)/shard_map/ppermute | solution.py:16
  7.2 0.7 %copy-start.3 = (f32[20,20]{1,0:T(8,128)S(1)}, f32[20,20]{1,0:T(8,128)}, u32[]{:S(2)}) copy-start(f32[20,20]{1,0:T(8,128)} %param.8) | copy-start | bytes 4804
  8.0 0.7 %copy-start.1 = (f32[4,4,1,1,1,1]{1,0,5,4,3,2:T(4,128)S(1)}, f32[4,4,1,1,1,1]{1,0,5,4,3,2:T(4,128)}, u32[]{:S(2)}) copy-start(f32[4,4,1,1,1,1]{1,0,5,4,3,2:T(4,128)} %constant.40) | copy-start | bytes 196
  16.0 4.3 %copy-start.2 = (f32[20,20]{1,0:T(8,128)S(1)}, f32[20,20]{1,0:T(8,128)}, u32[]{:S(2)}) copy-start(f32[20,20]{1,0:T(8,128)} %param.9) | copy-start | bytes 4804
  16.0 10.4 %collective-permute-start = (f32[4,1,20,128]{3,0,2,1:T(4,128)S(1)}, f32[4,1,20,128]{3,0,2,1:T(4,128)S(1)}, u32[]{:S(2)}, u32[]{:S(2)}) collective-permute-start(f32[4,1,20,128]{3,0,2,1:T(4,128)S(1)} %get-tuple-element.13), channel_id=1, source_target_pairs={{0,4},{4,8},{8,12},{12,16},{16,20},{20,24},{24,28},{28,0},{1,5},{5... | collective-permute-start | bytes 122888 | tf_op jit(solution)/shard_map/ppermute | solution.py:15
  16.0 10.3 %collective-permute-start.1 = (f32[4,1,20,128]{3,0,2,1:T(4,128)S(1)}, f32[4,1,20,128]{3,0,2,1:T(4,128)S(1)}, u32[]{:S(2)}, u32[]{:S(2)}) collective-permute-start(f32[4,1,20,128]{3,0,2,1:T(4,128)S(1)} %get-tuple-element.14), channel_id=1, source_target_pairs={{4,0},{8,4},{12,8},{16,12},{20,16},{24,20},{28,24},{0,28},{5,1},{9... | collective-permute-start | bytes 122888 | tf_op jit(solution)/shard_map/ppermute | solution.py:16
  20.3 3.6 %collective-permute-start.6 = (f32[1,22,1,1]{2,1,3,0:T(8,128)S(1)}, f32[1,22,1,1]{2,1,3,0:T(8,128)S(1)}, u32[]{:S(2)}, u32[]{:S(2)}) collective-permute-start(f32[1,22,1,1]{2,1,3,0:T(8,128)S(1)} %get-tuple-element.15), channel_id=1, source_target_pairs={{0,1},{1,2},{2,3},{3,0},{4,5},{5,6},{6,7},{7,4},{8,9},{9,10},{10,1... | collective-permute-start | bytes 272 | tf_op jit(solution)/shard_map/ppermute | solution.py:15
  23.1 3.1 %collective-permute-start.7 = (f32[1,22,1,1]{2,1,3,0:T(8,128)S(1)}, f32[1,22,1,1]{2,1,3,0:T(8,128)S(1)}, u32[]{:S(2)}, u32[]{:S(2)}) collective-permute-start(f32[1,22,1,1]{2,1,3,0:T(8,128)S(1)} %get-tuple-element.16), channel_id=1, source_target_pairs={{1,0},{2,1},{3,2},{0,3},{5,4},{6,5},{7,6},{4,7},{9,8},{10,9},{11,1... | collective-permute-start | bytes 272 | tf_op jit(solution)/shard_map/ppermute | solution.py:16
  26.4 1.3 %collective-permute-start.2 = (f32[4,22,1,128]{3,0,2,1:T(4,128)S(1)}, f32[4,22,1,128]{3,0,2,1:T(4,128)S(1)}, u32[]{:S(2)}, u32[]{:S(2)}) collective-permute-start(f32[4,22,1,128]{3,0,2,1:T(4,128)S(1)} %get-tuple-element.9), channel_id=1, source_target_pairs={{0,1},{1,2},{2,3},{3,0},{4,5},{5,6},{6,7},{7,4},{8,9},{9,10},{10,1... | collective-permute-start | bytes 135176 | tf_op jit(solution)/shard_map/ppermute | solution.py:15
  26.5 3.7 %collective-permute-start.3 = (f32[4,22,1,128]{3,0,2,1:T(4,128)S(1)}, f32[4,22,1,128]{3,0,2,1:T(4,128)S(1)}, u32[]{:S(2)}, u32[]{:S(2)}) collective-permute-start(f32[4,22,1,128]{3,0,2,1:T(4,128)S(1)} %get-tuple-element.10), channel_id=1, source_target_pairs={{1,0},{2,1},{3,2},{0,3},{5,4},{6,5},{7,6},{4,7},{9,8},{10,9},{11,1... | collective-permute-start | bytes 135176 | tf_op jit(solution)/shard_map/ppermute | solution.py:16
  38.9 5.6 %collective-permute-start.8 = (f32[4,1,20,128]{3,0,2,1:T(4,128)S(1)}, f32[4,1,20,128]{3,0,2,1:T(4,128)S(1)}, u32[]{:S(2)}, u32[]{:S(2)}) collective-permute-start(f32[4,1,20,128]{3,0,2,1:T(4,128)S(1)} %get-tuple-element.11), channel_id=1, source_target_pairs={{0,4},{4,8},{8,12},{12,16},{16,20},{20,24},{24,28},{28,0},{1,5},{5... | collective-permute-start | bytes 122888 | tf_op jit(solution)/shard_map/ppermute | solution.py:15
  38.9 5.5 %collective-permute-start.9 = (f32[4,1,20,128]{3,0,2,1:T(4,128)S(1)}, f32[4,1,20,128]{3,0,2,1:T(4,128)S(1)}, u32[]{:S(2)}, u32[]{:S(2)}) collective-permute-start(f32[4,1,20,128]{3,0,2,1:T(4,128)S(1)} %get-tuple-element.12), channel_id=1, source_target_pairs={{4,0},{8,4},{12,8},{16,12},{20,16},{24,20},{28,24},{0,28},{5,1},{9... | collective-permute-start | bytes 122888 | tf_op jit(solution)/shard_map/ppermute | solution.py:16
  44.5 2.3 %collective-permute-start.10 = (f32[4,22,1,128]{3,0,2,1:T(4,128)S(1)}, f32[4,22,1,128]{3,0,2,1:T(4,128)S(1)}, u32[]{:S(2)}, u32[]{:S(2)}) collective-permute-start(f32[4,22,1,128]{3,0,2,1:T(4,128)S(1)} %get-tuple-element.7), channel_id=1, source_target_pairs={{0,1},{1,2},{2,3},{3,0},{4,5},{5,6},{6,7},{7,4},{8,9},{9,10},{10,1... | collective-permute-start | bytes 135176 | tf_op jit(solution)/shard_map/ppermute | solution.py:15
  45.7 3.5 %collective-permute-start.11 = (f32[4,22,1,128]{3,0,2,1:T(4,128)S(1)}, f32[4,22,1,128]{3,0,2,1:T(4,128)S(1)}, u32[]{:S(2)}, u32[]{:S(2)}) collective-permute-start(f32[4,22,1,128]{3,0,2,1:T(4,128)S(1)} %get-tuple-element.8), channel_id=1, source_target_pairs={{1,0},{2,1},{3,2},{0,3},{5,4},{6,5},{7,6},{4,7},{9,8},{10,9},{11,1... | collective-permute-start | bytes 135176 | tf_op jit(solution)/shard_map/ppermute | solution.py:16
where the time goes:
time: 51.5 us; the launch traced here: 51.2 us
  starting transfers between devices  18 us (35%)
  matrix products  14 us (27%)
  waiting for transfers between devices  11.1 us (22%)
  local copies, waits for them, and re-layouts  4.25 us (8%)
  other arithmetic  3.59 us (7%)
    ppermute x6, starting transfers between devices, with_halo(): after = lax.ppermute(first, axis, down)  11.8 us
    ppermute x6, waiting for transfers between devices, with_halo(): after = lax.ppermute(first, axis, down)  7.12 us
    ppermute x6, starting transfers between devices, with_halo(): before = lax.ppermute(last, axis, up)  6.22 us
    ppermute x6, waiting for transfers between devices, with_halo(): before = lax.ppermute(last, axis, up)  3.99 us
    dot_general x2, matrix products, laplace(): grad_x = jnp.einsum('ab,febgcl->feagcl', table, shaped, precision=high)  3.99 us
    dot_general x2, matrix products, laplace(): weak = jnp.einsum('ba,febgcl->feagcl', table, flux_x, precision=high)  3.87 us
    dot_general x2, matrix products, laplace(): weak = weak + jnp.einsum('dc,febgdl->febgcl', table, flux_y, precision=high)  3.1 us
    dot_general x2, matrix products, laplace(): grad_y = jnp.einsum('cd,febgdl->febgcl', table, shaped, precision=high)  2.99 us
  transfers between devices with their start and end apart: 12, of which 7 were waited for; matrix products, arithmetic and copies ran while one was open for 18% of the time, Pallas kernels for 0%

commit v1 on v0

v1 whole, which is shorter than its diff:
```python
import functools

import jax
import jax.numpy as jnp
import numpy as np
from jax import lax
from jax.experimental import pallas as pl
from jax.experimental.pallas import tpu as pltpu
from jax.sharding import PartitionSpec as P

MESH = pl.DeviceIdType.MESH


def derivative_table():
    small = 1.0 / np.sqrt(5.0)
    nodes = np.array([-1.0, -small, small, 1.0])
    count = nodes.shape[0]
    weights = np.array(
        [np.prod([nodes[a] - nodes[k] for k in range(count) if k != a]) for a in range(count)]
    )
    table = np.zeros((count, count))
    for a in range(count):
        for b in range(count):
            if a == b:
                table[a, b] = np.sum([1.0 / (nodes[a] - nodes[k]) for k in range(count) if k != a])
            else:
                table[a, b] = weights[a] / weights[b] / (nodes[a] - nodes[b])
    return [[float(np.float32(v)) for v in row] for row in table]


def dot4(coefs, terms):
    total = None
    for c, t in zip(coefs, terms):
        if c == 0.0:
            continue
        total = c * t if total is None else total + c * t
    return total


def kernel(
    faces, cols, nf, nbx, nby, R,
    fields_hbm, diag_ref, cross_ref, mass_ref, out_hbm,
    raw, U, M, W, T, rmass,
    sR1, sC1, sK1, rR1, rC1, rK1, sR2, sC2, sK2, rR2, rC2, rK2,
    load_sem, store_sem, send_sem, recv_sem,
):
    face, col = lax.axis_index("face"), lax.axis_index("col")
    fside = (lax.rem(face + faces - 1, faces), lax.rem(face + 1, faces))
    cside = (lax.rem(col + cols - 1, cols), lax.rem(col + 1, cols))
    peers = [(fside[0], col), (fside[1], col), (face, cside[0]), (face, cside[1])]
    peers += [(fside[s], cside[t]) for s in range(2) for t in range(2)]

    loads = [
        pltpu.make_async_copy(fields_hbm.at[f], raw.at[f], load_sem.at[f]) for f in range(nf)
    ]
    for load in loads:
        load.start()
    barrier = pltpu.get_barrier_semaphore()
    for peer in peers:
        pl.semaphore_signal(barrier, inc=1, device_id=peer, device_id_type=MESH)

    D = derivative_table()
    lanes = raw.shape[-1]
    n = nbx * nby
    nx, ny = 4 * nbx, 4 * nby
    lead = up8(nby + 1)

    row = lax.broadcasted_iota(jnp.int32, (16 * R, 1), 0)
    a_of = sum((row >= 4 * R * k).astype(jnp.int32) for k in range(1, 4))
    rest = row - 4 * R * a_of
    j_of = sum((rest >= R * k).astype(jnp.int32) for k in range(1, 4))
    r_of = rest - R * j_of
    ex_of = sum((r_of >= nby * k).astype(jnp.int32) for k in range(1, nbx))
    ey_of = r_of - nby * ex_of
    valid = r_of < n
    x_at = lax.broadcasted_iota(jnp.int32, (16 * R, nx), 1)
    y_at = lax.broadcasted_iota(jnp.int32, (16 * R, ny), 1)
    pick_x = jnp.where((x_at == 4 * ex_of + a_of) & valid, 1.0, 0.0).astype(jnp.bfloat16)
    keep_y = jnp.where(y_at == 4 * ey_of + j_of, 1.0, 0.0)
    ones = jnp.ones((ny, lanes), jnp.bfloat16)

    def planes(m):
        total = None
        for _ in range(3):
            part = m.astype(jnp.bfloat16)
            m = m - part.astype(jnp.float32)
            rows = jnp.dot(pick_x, part, preferred_element_type=jnp.float32) * keep_y
            wide = jnp.dot(rows.astype(jnp.bfloat16), ones, preferred_element_type=jnp.float32)
            total = wide if total is None else total + wide
        return total.reshape(4, 4, R, lanes)

    M[0] = planes(diag_ref[0])
    M[1] = planes(cross_ref[...])
    M[2] = planes(diag_ref[1])
    W[:, :, pl.ds(lead + nf * R, R), :] = planes(mass_ref[...])
    for at in (0, lead + (nf + 1) * R):
        W[:, :, pl.ds(at, lead), :] = jnp.zeros((4, 4, lead, lanes), jnp.float32)

    r_one = lax.broadcasted_iota(jnp.int32, (R, lanes), 0)
    ey_one = r_one - nby * sum((r_one >= nby * k).astype(jnp.int32) for k in range(1, nbx))
    inside = r_one < n
    low = jnp.where(inside & (ey_one > 0), 1.0, 0.0)
    high = jnp.where(inside & (ey_one < nby - 1), 1.0, 0.0)

    pad = n // 8 * 8
    for f in range(nf):
        for a in range(4):
            for j in range(4):
                U[a, j, pl.ds(f * R + pad, R - pad), :] = jnp.zeros((R - pad, lanes), jnp.float32)
    for f in range(nf):
        loads[f].wait()
        for ex in range(nbx):
            for a in range(4):
                for j in range(4):
                    U[a, j, pl.ds(f * R + nby * ex, nby), :] = raw[
                        f, 4 * ex + a, pl.ds(j, nby, stride=4), :
                    ]

    def laplace(f, carry):
        for rb in range(R // 8):
            at = pl.ds(pl.multiple_of(f * R + rb * 8, 8), 8)
            mat = pl.ds(rb * 8, 8)
            u = [[U[a, j, at, :] for j in range(4)] for a in range(4)]
            fx = [[None] * 4 for _ in range(4)]
            fy = [[None] * 4 for _ in range(4)]
            for a in range(4):
                for j in range(4):
                    gx = dot4(D[a], [u[b][j] for b in range(4)])
                    gy = dot4(D[j], [u[a][d] for d in range(4)])
                    m0, mc, m1 = M[0, a, j, mat, :], M[1, a, j, mat, :], M[2, a, j, mat, :]
                    fx[a][j] = m0 * gx + mc * gy
                    fy[a][j] = mc * gx + m1 * gy
            wat = pl.ds(pl.multiple_of(f * R + rb * 8 + lead, 8), 8)
            for a in range(4):
                for j in range(4):
                    W[a, j, wat, :] = dot4(
                        [-D[b][a] for b in range(4)], [fx[b][j] for b in range(4)]
                    ) + dot4([-D[d][j] for d in range(4)], [fy[a][d] for d in range(4)])
        return carry

    def partial_assemble(f):
        def w(a, j, shift):
            return W[a, j, pl.ds(lead + f * R + shift, R), :]

        def s(a, j, shift):
            if a == 0:
                return w(0, j, shift) + w(3, j, shift - nby)
            if a == 3:
                return w(3, j, shift) + w(0, j, shift + nby)
            return w(a, j, shift)

        at = pl.ds(f * R, R)
        for a in range(4):
            T[a, 0, at, :] = s(a, 0, 0) + low * s(a, 3, -1)
            T[a, 1, at, :] = s(a, 1, 0)
            T[a, 2, at, :] = s(a, 2, 0)
            T[a, 3, at, :] = s(a, 3, 0) + high * s(a, 0, 1)

    def exchange(phase, count, sR, sC, sK, rR, rC, rK):
        wx, wy = count * nby, count * nbx
        for d in range(2):
            e = 3 * d
            for f in range(count):
                for k in range(4):
                    sR[d, pl.ds(k * wx + f * nby, nby), :] = T[
                        e, k, pl.ds(f * R + d * (nbx - 1) * nby, nby), :
                    ]
                    sC[d, pl.ds(k * wy + f * nbx, nbx), :] = T[
                        k, e, pl.ds(f * R + d * (nby - 1), nbx, stride=nby), :
                    ]
        for s in range(2):
            for t in range(2):
                start = s * (nbx - 1) * nby + t * (nby - 1)
                for f in range(count):
                    sK[2 * s + t, pl.ds(f, 1), :] = T[3 * s, 3 * t, pl.ds(f * R + start, 1), :]
        pairs = [(sR.at[d], rR.at[1 - d]) for d in range(2)]
        pairs += [(sC.at[d], rC.at[1 - d]) for d in range(2)]
        pairs += [(sK.at[k], rK.at[3 - k]) for k in range(4)]
        copies = []
        for k, (src, dst) in enumerate(pairs):
            back = k ^ 1 if k < 4 else 11 - k
            copies.append(
                pltpu.make_async_remote_copy(
                    src_ref=src, dst_ref=dst,
                    send_sem=send_sem.at[phase, k], recv_sem=recv_sem.at[phase, back],
                    device_id=peers[k], device_id_type=MESH,
                )
            )
            copies[-1].start()
        return copies

    def finish(copies, count, rR, rC, rK):
        wx, wy = count * nby, count * nbx
        for copy in copies:
            copy.wait_recv()
        for d in range(2):
            e = 3 * d
            for f in range(count):
                for k in range(4):
                    at = pl.ds(f * R + d * (nbx - 1) * nby, nby)
                    T[e, k, at, :] = T[e, k, at, :] + rR[d, pl.ds(k * wx + f * nby, nby), :]
        for d in range(2):
            e = 3 * d
            for f in range(count):
                for k in range(4):
                    at = pl.ds(f * R + d * (nby - 1), nbx, stride=nby)
                    T[k, e, at, :] = T[k, e, at, :] + rC[d, pl.ds(k * wy + f * nbx, nbx), :]
        for s in range(2):
            for t in range(2):
                start = s * (nbx - 1) * nby + t * (nby - 1)
                for f in range(count):
                    at = pl.ds(f * R + start, 1)
                    T[3 * s, 3 * t, at, :] = (
                        T[3 * s, 3 * t, at, :] + rK[2 * s + t, pl.ds(f, 1), :]
                    )

    lax.fori_loop(0, nf, laplace, 0)
    for f in range(nf + 1):
        partial_assemble(f)
    pl.semaphore_wait(barrier, len(peers))
    first_copies = exchange(0, nf + 1, sR1, sC1, sK1, rR1, rC1, rK1)
    finish(first_copies, nf + 1, rR1, rC1, rK1)
    for a in range(4):
        for j in range(4):
            total = T[a, j, pl.ds(nf * R, R), :]
            scale = jnp.where(inside, 1.0 / jnp.where(inside, total, 1.0), 0.0)
            rmass[a, j] = scale
            for f in range(nf):
                U[a, j, pl.ds(f * R, R), :] = T[a, j, pl.ds(f * R, R), :] * scale

    lax.fori_loop(0, nf, laplace, 0)
    for f in range(nf):
        partial_assemble(f)
    second_copies = exchange(1, nf, sR2, sC2, sK2, rR2, rC2, rK2)
    finish(second_copies, nf, rR2, rC2, rK2)
    stores = []
    for f in range(nf):
        for ex in range(nbx):
            for a in range(4):
                for j in range(4):
                    raw[f, 4 * ex + a, pl.ds(j, nby, stride=4), :] = (
                        T[a, j, pl.ds(f * R + nby * ex, nby), :]
                        * rmass[a, j, pl.ds(nby * ex, nby), :]
                    )
        stores.append(pltpu.make_async_copy(raw.at[f], out_hbm.at[f], store_sem.at[f]))
        stores[-1].start()
    for copy in first_copies + second_copies:
        copy.wait_send()
    for store in stores:
        store.wait()


def up8(count):
    return -(-count // 8) * 8


def solution(mesh):
    faces, cols = mesh.shape["face"], mesh.shape["col"]

    def shards(fields, metric_diag, metric_cross, point_mass):
        nf, rows, width, lanes = fields.shape
        nbx, nby = rows // 4, width // 4
        R = up8(nbx * nby + nby + 1)
        f32 = jnp.float32

        def vmem(*shape):
            return pltpu.VMEM(shape, f32)

        def edges(count):
            return [
                vmem(2, up8(4 * count * nby), lanes),
                vmem(2, up8(4 * count * nbx), lanes),
                vmem(4, up8(count), lanes),
            ]

        return pl.pallas_call(
            functools.partial(kernel, faces, cols, nf, nbx, nby, R),
            out_shape=jax.ShapeDtypeStruct(fields.shape, f32),
            in_specs=[pl.BlockSpec(memory_space=pl.ANY)]
            + [pl.BlockSpec(memory_space=pltpu.VMEM)] * 3,
            out_specs=pl.BlockSpec(memory_space=pl.ANY),
            scratch_shapes=[
                vmem(nf, rows, width, lanes),
                vmem(4, 4, nf * R, lanes),
                vmem(3, 4, 4, R, lanes),
                vmem(4, 4, 2 * up8(nby + 1) + (nf + 1) * R, lanes),
                vmem(4, 4, (nf + 1) * R, lanes),
                vmem(4, 4, R, lanes),
                *edges(nf + 1), *edges(nf + 1), *edges(nf), *edges(nf),
                pltpu.SemaphoreType.DMA((nf,)),
                pltpu.SemaphoreType.DMA((nf,)),
                pltpu.SemaphoreType.DMA((2, 8)),
                pltpu.SemaphoreType.DMA((2, 8)),
            ],
            compiler_params=pltpu.CompilerParams(
                collective_id=0, has_side_effects=True, vmem_limit_bytes=32 * 1024 * 1024
            ),
        )(fields, metric_diag, metric_cross, point_mass)

    return jax.shard_map(
        shards,
        mesh=mesh,
        in_specs=(
            P(None, "face", "col", None),
            P(None, "face", "col"),
            P("face", "col"),
            P("face", "col"),
        ),
        out_specs=P(None, "face", "col", None),
        check_vma=False,
    )
```

time: 51.5 us -> 22.4 us (0.43)
  Pallas kernels: 0 us -> 18.6 us
  starting transfers between devices: 18 us -> 0 us
  matrix products: 14 us -> 0 us
  waiting for transfers between devices: 11.1 us -> 0 us
  other arithmetic: 3.59 us -> 0 us
  local copies, waits for them, and re-layouts: 4.25 us -> 3.41 us
    pallas_call x0 -> x1, Pallas kernels: none -> 18.6 us  [shards(): pl.pallas_call(functools.partial(kernel, faces, cols, nf, nbx, nby, R), o...]
    ppermute x12 -> x0, starting transfers between devices: 18 us -> none  [the longest x6 11.8 us: with_halo(): after = lax.ppermute(first, axis, down)]
    dot_general x8 -> x0, matrix products: 14 us -> none  [the longest x2 3.99 us: laplace(): grad_x = jnp.einsum('ab,febgcl->feagcl', table, shaped, precision=high)]
    ppermute x12 -> x0, waiting for transfers between devices: 11.1 us -> none  [the longest x6 7.12 us: with_halo(): after = lax.ppermute(first, axis, down)]
    div x3 -> x0, other arithmetic: 2.28 us -> none  [the longest x1 1.47 us: shards(): return assemble(padded_second) / mass_sum]
    slice x5 -> x0, local copies, waits for them, and re-layouts: 1.73 us -> none  [the longest x4 0.87 us: with_halo(): last = lax.slice_in_dim(array, length - width, length, axis=dim)]
    pallas_call x0 -> x1, local copies, waits for them, and re-layouts: none -> 1.42 us  [shards(): pl.pallas_call(functools.partial(kernel, faces, cols, nf, nbx, nby, R), o...]
    unnamed x8 -> x6, local copies, waits for them, and re-layouts: 0.86 us -> 1.99 us
  transfers between devices with their start and end apart: 12 -> 0, of which waited for: 7 -> 0; matrix products, arithmetic and copies ran while one was open for 18% -> 0% of each run, Pallas kernels for 0% -> 0%
where the time goes in v1:
time: 22.4 us; the launch traced here: 22.1 us
  Pallas kernels  18.6 us (83%)
  local copies, waits for them, and re-layouts  3.41 us (15%)
    pallas_call x1, Pallas kernels, shards(): pl.pallas_call(functools.partial(kernel, faces, cols, nf, nbx, nby, R), o...  18.6 us
    unnamed x6, local copies, waits for them, and re-layouts  1.99 us
    pallas_call x1, local copies, waits for them, and re-layouts, shards(): pl.pallas_call(functools.partial(kernel, faces, cols, nf, nbx, nby, R), o...  1.42 us

profile of v1, /device:TPU:1, one launch (start us, length us, event | category | flops | bytes accessed | tf_op | source)
XLA Modules:
  0.0 22.1 jit_solution(8486120812571189659)
XLA Ops:
  0.0 0.7 %copy.6.diag_ref = f32[2,20,20]{2,1,0:T(8,128)S(1)} copy(f32[2,20,20]{2,0,1:T(2,128)} %param.5) | data formatting | bytes 6400 | tf_op args[1]
  0.7 0.0 copy-start
  0.7 0.0 copy-start.1
  0.7 1.3 %copy.5.fields_hbm = f32[4,20,20,128]{3,2,1,0:T(8,128)S(1)} copy(f32[4,20,20,128]{3,0,2,1:T(4,128)} %param.4) | data formatting | bytes 1638400 | tf_op args[0]
  2.0 0.0 copy-done
  2.0 0.0 copy-done.1
  2.0 18.6 %shard_map.46 = f32[4,20,20,128]{3,2,1,0:T(8,128)S(1)} custom-call(f32[4,20,20,128]{3,2,1,0:T(8,128)S(1)} %copy.5.fields_hbm, f32[2,20,20]{2,1,0:T(8,128)S(1)} %copy.6.diag_ref, f32[20,20]{1,0:T(8,128)S(1)} %copy-done, f32[20,20]{1,0:T(8,128)S(1)} %copy-done.1), custom_call_target="tpu_custom_call" | custom-call | tf_op jit(solution)/shard_map/pallas_call | solution.py:276
  20.7 1.4 %copy.7 = f32[4,20,20,128]{3,0,2,1:T(4,128)} copy(f32[4,20,20,128]{3,2,1,0:T(8,128)S(1)} %shard_map.46) | data formatting | bytes 1638400 | tf_op jit(solution)/shard_map/pallas_call | solution.py:276
Async XLA Ops:
  0.7 1.3 %copy-start = (f32[20,20]{1,0:T(8,128)S(1)}, f32[20,20]{1,0:T(8,128)}, u32[]{:S(2)}) copy-start(f32[20,20]{1,0:T(8,128)} %cross_ref.1) | copy-start | bytes 4804
  0.7 1.3 %copy-start.1 = (f32[20,20]{1,0:T(8,128)S(1)}, f32[20,20]{1,0:T(8,128)}, u32[]{:S(2)}) copy-start(f32[20,20]{1,0:T(8,128)} %mass_ref.1) | copy-start | bytes 4804

commit v2 on v0

v2 whole, which is shorter than its diff:
```python
import functools

import jax
import jax.numpy as jnp
import numpy as np
from jax import lax
from jax.experimental import pallas as pl
from jax.experimental.pallas import tpu as pltpu
from jax.sharding import PartitionSpec as P

MESH = pl.DeviceIdType.MESH


def derivative_table():
    small = 1.0 / np.sqrt(5.0)
    nodes = np.array([-1.0, -small, small, 1.0])
    count = nodes.shape[0]
    weights = np.array(
        [np.prod([nodes[a] - nodes[k] for k in range(count) if k != a]) for a in range(count)]
    )
    table = np.zeros((count, count))
    for a in range(count):
        for b in range(count):
            if a == b:
                table[a, b] = np.sum([1.0 / (nodes[a] - nodes[k]) for k in range(count) if k != a])
            else:
                table[a, b] = weights[a] / weights[b] / (nodes[a] - nodes[b])
    return [[float(np.float32(v)) for v in row] for row in table]


def dot4(coefs, terms):
    total = None
    for c, t in zip(coefs, terms):
        if isinstance(c, float) and c == 0.0:
            continue
        total = c * t if total is None else total + c * t
    return total


def kernel(
    faces, cols, nf, nbx, nby,
    fields_hbm, diag_ref, cross_ref, mass_ref, out_ref,
    raw, U, M, W, T, spread, rM,
    sC1, rR1, rC1, rK1, sC2, rR2, rC2, rK2,
    load_sem, mass_send, mass_recv, send_sem, recv_sem,
):
    face, col = lax.axis_index("face"), lax.axis_index("col")
    fside = (lax.rem(face + faces - 1, faces), lax.rem(face + 1, faces))
    cside = (lax.rem(col + cols - 1, cols), lax.rem(col + 1, cols))
    peers = [(fside[0], col), (fside[1], col), (face, cside[0]), (face, cside[1])]
    peers += [(fside[s], cside[t]) for s in range(2) for t in range(2)]
    opposite = [1, 0, 3, 2, 7, 6, 5, 4]

    nx, ny, nq = 4 * nbx, 4 * nby, 2 * nby
    lanes = raw.shape[-1]
    order = [0, nbx - 1] + list(range(1, nbx - 1))
    loads = {
        ex: pltpu.make_async_copy(
            fields_hbm.at[pl.ds(4 * ex, 4)], raw.at[pl.ds(4 * ex, 4)], load_sem.at[ex]
        )
        for ex in order
    }
    for ex in order:
        loads[ex].start()
    barrier = pltpu.get_barrier_semaphore()
    for peer in peers:
        pl.semaphore_signal(barrier, inc=1, device_id=peer, device_id_type=MESH)

    D = derivative_table()
    sub = lax.broadcasted_iota(jnp.int32, (2 * nf, lanes), 0)
    is_low = sub < nf
    low = jnp.where(is_low, 1.0, 0.0)
    high = 1.0 - low

    def swap(v):
        return pltpu.roll(v, nf, 0)

    def halves(table):
        return [
            [
                jnp.where(is_low, table[2 * p][2 * q + k], table[2 * p + 1][2 * q + 1 - k])
                for q in range(2) for k in range(2)
            ]
            for p in range(2)
        ]

    minus_t = [[-D[b][a] for b in range(4)] for a in range(4)]
    D_half, minus_half = halves(D), halves(minus_t)

    row = lax.broadcasted_iota(jnp.int32, (nf * ny, 3 * ny), 0)
    lane = lax.broadcasted_iota(jnp.int32, (nf * ny, 3 * ny), 1)
    keep = jnp.zeros((nf * ny, 3 * ny), jnp.float32)
    for k in range(3):
        first_row = nf * (lane - k * ny)
        keep = jnp.where((row >= first_row) & (row < first_row + nf), 1.0, keep)
    ones = jnp.ones((3 * ny, lanes), jnp.bfloat16)

    def split(slot, m):
        parts = []
        for _ in range(3):
            part = m.astype(jnp.bfloat16).astype(jnp.float32)
            m = m - part
            parts.append(part)
        spread[slot] = jnp.concatenate(parts, axis=1)

    def spread_row(slot, x):
        left = (keep * spread[slot, pl.ds(x, 1), :]).astype(jnp.bfloat16)
        wide = jnp.dot(left, ones, preferred_element_type=jnp.float32)
        M[slot, x] = wide.reshape(nq, 2 * nf, lanes)

    split(0, diag_ref[0])
    split(1, cross_ref[...])
    split(2, diag_ref[1])
    for x in range(nx):
        for slot in range(3):
            spread_row(slot, x)

    def laplace(src, ex, ey):
        u = [[src[4 * ex + a, 2 * ey + p] for p in range(2)] for a in range(4)]
        fx = [[None] * 2 for _ in range(4)]
        fy = [[None] * 2 for _ in range(4)]
        for a in range(4):
            mix = [u[a][0], swap(u[a][0]), u[a][1], swap(u[a][1])]
            for p in range(2):
                at = (4 * ex + a, 2 * ey + p)
                gx = dot4(D[a], [u[b][p] for b in range(4)])
                gy = dot4(D_half[p], mix)
                m0, mc, m1 = M[(0,) + at], M[(1,) + at], M[(2,) + at]
                fx[a][p] = m0 * gx + mc * gy
                fy[a][p] = mc * gx + m1 * gy
        for a in range(4):
            mix = [fy[a][0], swap(fy[a][0]), fy[a][1], swap(fy[a][1])]
            for p in range(2):
                W[4 * ex + a, 2 * ey + p] = dot4(
                    minus_t[a], [fx[b][p] for b in range(4)]
                ) + dot4(minus_half[p], mix)

    def rows_sum(x, q):
        if x % 4 == 0 and x > 0:
            return W[x, q] + W[x - 1, q]
        if x % 4 == 3 and x < nx - 1:
            return W[x, q] + W[x + 1, q]
        return W[x, q]

    def assemble_row(x):
        line = [rows_sum(x, q) for q in range(nq)]
        for ey in range(1, nby):
            v, w = line[2 * ey - 1], line[2 * ey]
            line[2 * ey - 1], line[2 * ey] = v + high * swap(w), w + low * swap(v)
        for q in range(nq):
            T[x, q] = line[q]
            if x % 4 == 3 and x < nx - 1:
                T[x + 1, q] = line[q]

    def send(phase, k, src, dst):
        copy = pltpu.make_async_remote_copy(
            src_ref=src, dst_ref=dst,
            send_sem=send_sem.at[phase, k], recv_sem=recv_sem.at[phase, opposite[k]],
            device_id=peers[k], device_id_type=MESH,
        )
        copy.start()
        return copy

    def phase_sends(phase, src, sC, rR, rC, rK, ready):
        copies = [None] * 8
        for ex in order[:2]:
            ready(ex)
            for ey in range(nby):
                laplace(src, ex, ey)
        for x in (0, nx - 1):
            assemble_row(x)
        if phase == 0:
            pl.semaphore_wait(barrier, len(peers))
        for s in range(2):
            for t in range(2):
                k = 4 + 2 * s + t
                copies[k] = send(
                    phase, k, W.at[s * (nx - 1), t * (nq - 1)], rK.at[3 - 2 * s - t]
                )
        for s in range(2):
            copies[s] = send(phase, s, T.at[s * (nx - 1)], rR.at[1 - s])
        if phase == 0:
            for k in range(8):
                masses.append(
                    pltpu.make_async_remote_copy(
                        src_ref=mass_ref, dst_ref=rM.at[opposite[k]],
                        send_sem=mass_send.at[k], recv_sem=mass_recv.at[opposite[k]],
                        device_id=peers[k], device_id_type=MESH,
                    )
                )
                masses[-1].start()
        for ex in order[2:]:
            ready(ex)
            for ey in range(nby):
                laplace(src, ex, ey)
        for k in range(nx // 2):
            a, b = rows_sum(2 * k, 0), rows_sum(2 * k + 1, 0)
            sC[0, k] = jnp.where(is_low, a, swap(b))
            a, b = rows_sum(2 * k, nq - 1), rows_sum(2 * k + 1, nq - 1)
            sC[1, k] = jnp.where(is_low, swap(a), b)
        for t in range(2):
            copies[2 + t] = send(phase, 2 + t, sC.at[t], rC.at[1 - t])
        for x in range(1, nx - 1):
            if x % 4 != 0:
                assemble_row(x)
        return copies

    def finished(x, rR, rC, rK):
        line = [T[x, q] for q in range(nq)]
        if x in (0, nx - 1):
            s = 0 if x == 0 else 1
            line = [v + rR[s, q] for q, v in enumerate(line)]
            line[0] = line[0] + low * swap(rK[2 * s])
            line[-1] = line[-1] + high * swap(rK[2 * s + 1])
        before, after = rC[0, x // 2], rC[1, x // 2]
        if x % 2 == 0:
            after = swap(after)
        else:
            before = swap(before)
        line[0] = line[0] + low * before
        line[-1] = line[-1] + high * after
        return line

    masses = []
    first_copies = phase_sends(0, raw, sC1, rR1, rC1, rK1, lambda ex: loads[ex].wait())

    for copy in masses:
        copy.wait_recv()
    x_at = lax.broadcasted_iota(jnp.int32, (nx, ny), 0)
    y_at = lax.broadcasted_iota(jnp.int32, (nx, ny), 1)
    x_low, x_high = (x_at & 3) == 0, (x_at & 3) == 3
    y_low, y_high = (y_at & 3) == 0, (y_at & 3) == 3

    def mass_rows(own, prev, nxt):
        down = jnp.concatenate([prev[nx - 1:], own[: nx - 1]], axis=0)
        up = jnp.concatenate([own[1:], nxt[:1]], axis=0)
        return own + jnp.where(x_low, down, 0.0) + jnp.where(x_high, up, 0.0)

    here = mass_rows(mass_ref[...], rM[0], rM[1])
    left = mass_rows(rM[2], rM[4], rM[6])
    right = mass_rows(rM[3], rM[5], rM[7])
    back = jnp.concatenate([left[:, ny - 1:], here[:, : ny - 1]], axis=1)
    ahead = jnp.concatenate([here[:, 1:], right[:, :1]], axis=1)
    mass_sum = here + jnp.where(y_low, back, 0.0) + jnp.where(y_high, ahead, 0.0)
    split(3, 1.0 / mass_sum)
    for x in range(nx):
        spread_row(3, x)

    for copy in first_copies:
        copy.wait_recv()
    for x in range(nx):
        line = finished(x, rR1, rC1, rK1)
        for q in range(nq):
            U[x, q] = line[q] * M[3, x, q]
    for copy in first_copies:
        copy.wait_send()

    second_copies = phase_sends(1, U, sC2, rR2, rC2, rK2, lambda ex: None)
    for copy in second_copies:
        copy.wait_recv()
    for x in range(nx):
        line = finished(x, rR2, rC2, rK2)
        for q in range(nq):
            out_ref[x, q] = line[q] * M[3, x, q]
    for copy in second_copies + masses:
        copy.wait_send()


def solution(mesh):
    faces, cols = mesh.shape["face"], mesh.shape["col"]

    def shards(fields, metric_diag, metric_cross, point_mass):
        nf, nx, ny, lanes = fields.shape
        nbx, nby = nx // 4, ny // 4
        f32 = jnp.float32
        tiles = (nx, ny // 2, 2 * nf, lanes)

        def vmem(*shape):
            return pltpu.VMEM(shape, f32)

        def landing():
            return [
                vmem(2, nx // 2, 2 * nf, lanes),
                vmem(2, ny // 2, 2 * nf, lanes),
                vmem(2, nx // 2, 2 * nf, lanes),
                vmem(4, 2 * nf, lanes),
            ]

        out = pl.pallas_call(
            functools.partial(kernel, faces, cols, nf, nbx, nby),
            out_shape=jax.ShapeDtypeStruct(tiles, f32),
            in_specs=[pl.BlockSpec(memory_space=pl.ANY)]
            + [pl.BlockSpec(memory_space=pltpu.VMEM)] * 3,
            out_specs=pl.BlockSpec(memory_space=pltpu.VMEM),
            scratch_shapes=[
                vmem(*tiles),
                vmem(*tiles),
                vmem(4, *tiles),
                vmem(*tiles),
                vmem(*tiles),
                vmem(4, nx, 3 * ny),
                vmem(8, nx, ny),
                *landing(), *landing(),
                pltpu.SemaphoreType.DMA((nbx,)),
                pltpu.SemaphoreType.DMA((8,)),
                pltpu.SemaphoreType.DMA((8,)),
                pltpu.SemaphoreType.DMA((2, 8)),
                pltpu.SemaphoreType.DMA((2, 8)),
            ],
            compiler_params=pltpu.CompilerParams(
                collective_id=0, has_side_effects=True, vmem_limit_bytes=32 * 1024 * 1024
            ),
        )(
            fields.transpose(1, 2, 0, 3).reshape(tiles),
            metric_diag, metric_cross, point_mass,
        )
        return out.reshape(nx, ny, nf, lanes).transpose(2, 0, 1, 3)

    return jax.shard_map(
        shards,
        mesh=mesh,
        in_specs=(
            P(None, "face", "col", None),
            P(None, "face", "col"),
            P("face", "col"),
            P("face", "col"),
        ),
        out_specs=P(None, "face", "col", None),
        check_vma=False,
    )
```

time: 51.5 us -> 22 us (0.43)
  Pallas kernels: 0 us -> 18.8 us
  starting transfers between devices: 18 us -> 0 us
  matrix products: 14 us -> 0 us
  waiting for transfers between devices: 11.1 us -> 0 us
  other arithmetic: 3.59 us -> 0 us
  local copies, waits for them, and re-layouts: 4.25 us -> 2.79 us
    pallas_call x0 -> x1, Pallas kernels: none -> 18.8 us  [shards(): pl.pallas_call(functools.partial(kernel, faces, cols, nf, nbx, nby), out_...]
    ppermute x12 -> x0, starting transfers between devices: 18 us -> none  [the longest x6 11.8 us: with_halo(): after = lax.ppermute(first, axis, down)]
    dot_general x8 -> x0, matrix products: 14 us -> none  [the longest x2 3.99 us: laplace(): grad_x = jnp.einsum('ab,febgcl->feagcl', table, shaped, precision=high)]
    ppermute x12 -> x0, waiting for transfers between devices: 11.1 us -> none  [the longest x6 7.12 us: with_halo(): after = lax.ppermute(first, axis, down)]
    div x3 -> x0, other arithmetic: 2.28 us -> none  [the longest x1 1.47 us: shards(): return assemble(padded_second) / mass_sum]
    unnamed x8, local copies, waits for them, and re-layouts: 0.86 us -> 2.79 us
    slice x5 -> x0, local copies, waits for them, and re-layouts: 1.73 us -> none  [the longest x4 0.87 us: with_halo(): last = lax.slice_in_dim(array, length - width, length, axis=dim)]
    mul x6 -> x0, local copies, waits for them, and re-layouts: 1.02 us -> none  [the longest x4 0.68 us: laplace(): flux_x = first_diag * grad_x + cross_term * grad_y]
  transfers between devices with their start and end apart: 12 -> 0, of which waited for: 7 -> 0; matrix products, arithmetic and copies ran while one was open for 18% -> 0% of each run, Pallas kernels for 0% -> 0%
where the time goes in v2:
time: 22 us; the launch traced here: 21.6 us
  Pallas kernels  18.8 us (85%)
  local copies, waits for them, and re-layouts  2.79 us (13%)
    pallas_call x1, Pallas kernels, shards(): pl.pallas_call(functools.partial(kernel, faces, cols, nf, nbx, nby), out_...  18.8 us
    unnamed x8, local copies, waits for them, and re-layouts  2.79 us

profile of v2, /device:TPU:1, one launch (start us, length us, event | category | flops | bytes accessed | tf_op | source)
XLA Modules:
  0.0 21.6 jit_solution(15306638310891589113)
XLA Ops:
  0.0 0.0 copy-start.1
  0.0 0.0 copy-start.2
  0.0 0.8 %copy.5.diag_ref = f32[2,20,20]{2,1,0:T(8,128)S(1)} copy(f32[2,20,20]{2,0,1:T(2,128)} %param.5) | data formatting | bytes 6400 | tf_op args[1]
  0.8 0.0 copy-done.1
  0.8 0.0 copy-done.2
  0.8 0.0 copy-start
  0.8 1.1 %copy-done = f32[4,20,20,128]{3,0,2,1:T(4,128)S(1)} copy-done((f32[4,20,20,128]{3,0,2,1:T(4,128)S(1)}, f32[4,20,20,128]{3,0,2,1:T(4,128)}, u32[]{:S(2)}) %copy-start) | copy-done | bytes 819224
  1.9 18.8 %shard_map.46 = f32[20,10,8,128]{3,2,1,0:T(8,128)S(1)} custom-call(f32[20,10,8,128]{3,2,1,0:T(8,128)S(1)} %bitcast.7, f32[2,20,20]{2,1,0:T(8,128)S(1)} %copy.5.diag_ref, f32[20,20]{1,0:T(8,128)S(1)} %copy-done.1, f32[20,20]{1,0:T(8,128)S(1)} %copy-done.2), custom_call_target="tpu_custom_call" | custom-call | tf_op jit(solution)/shard_map/pallas_call | solution.py:289
  20.7 0.9 %copy.7 = f32[4,20,20,128]{3,0,2,1:T(4,128)} copy(f32[4,20,20,128]{3,0,2,1:T(4,128)S(1)} %bitcast.6) | data formatting | bytes 1638400
Async XLA Ops:
  0.0 0.8 %copy-start.1 = (f32[20,20]{1,0:T(8,128)S(1)}, f32[20,20]{1,0:T(8,128)}, u32[]{:S(2)}) copy-start(f32[20,20]{1,0:T(8,128)} %cross_ref.1) | copy-start | bytes 4804
  0.0 0.8 %copy-start.2 = (f32[20,20]{1,0:T(8,128)S(1)}, f32[20,20]{1,0:T(8,128)}, u32[]{:S(2)}) copy-start(f32[20,20]{1,0:T(8,128)} %mass_ref.1) | copy-start | bytes 4804
  0.8 1.1 %copy-start = (f32[4,20,20,128]{3,0,2,1:T(4,128)S(1)}, f32[4,20,20,128]{3,0,2,1:T(4,128)}, u32[]{:S(2)}) copy-start(f32[4,20,20,128]{3,0,2,1:T(4,128)} %param.4) | copy-start | bytes 2457604

commit v3 on v2

--- a/solution.py
+++ b/solution.py
@@ -40,8 +40,8 @@
 def kernel(
     faces, cols, nf, nbx, nby,
     fields_hbm, diag_ref, cross_ref, mass_ref, out_ref,
-    raw, U, M, W, T, spread, rM,
-    sC1, rR1, rC1, rK1, sC2, rR2, rC2, rK2,
+    raw, U, M, W, T, spread, sM, rM,
+    sC1, sK1, rR1, rC1, rK1, sC2, sK2, rR2, rC2, rK2,
     load_sem, mass_send, mass_recv, send_sem, recv_sem,
 ):
     face, col = lax.axis_index("face"), lax.axis_index("col")
@@ -66,6 +66,17 @@
     for peer in peers:
         pl.semaphore_signal(barrier, inc=1, device_id=peer, device_id_type=MESH)
 
+    square_x = lax.broadcasted_iota(jnp.int32, (nx, nx), 0)
+    square_y = lax.broadcasted_iota(jnp.int32, (nx, nx), 1)
+    diagonal = square_x == square_y
+    sM[pl.ds(0, 1), pl.ds(0, ny)] = mass_ref[pl.ds(0, 1), :]
+    sM[pl.ds(1, 1), pl.ds(0, ny)] = mass_ref[pl.ds(nx - 1, 1), :]
+    for t in range(2):
+        column = mass_ref[:, pl.ds(t * (ny - 1), 1)]
+        sM[pl.ds(2 + t, 1), pl.ds(0, nx)] = jnp.sum(
+            jnp.where(diagonal, column, 0.0), axis=0, keepdims=True
+        )
+
     D = derivative_table()
     sub = lax.broadcasted_iota(jnp.int32, (2 * nf, lanes), 0)
     is_low = sub < nf
@@ -108,12 +119,15 @@
         wide = jnp.dot(left, ones, preferred_element_type=jnp.float32)
         M[slot, x] = wide.reshape(nq, 2 * nf, lanes)
 
-    split(0, diag_ref[0])
+    split(0, diag_ref[:, 0, :])
     split(1, cross_ref[...])
-    split(2, diag_ref[1])
-    for x in range(nx):
+    split(2, diag_ref[:, 1, :])
+    def spread_metrics(x, carry):
         for slot in range(3):
             spread_row(slot, x)
+        return carry
+
+    lax.fori_loop(0, nx, spread_metrics, 0)
 
     def laplace(src, ex, ey):
         u = [[src[4 * ex + a, 2 * ey + p] for p in range(2)] for a in range(4)]
@@ -161,29 +175,36 @@
         copy.start()
         return copy
 
-    def phase_sends(phase, src, sC, rR, rC, rK, ready):
+    def corner(s, t):
+        tile = W[s * (nx - 1), t * (nq - 1)]
+        return tile[t * nf:(t + 1) * nf]
+
+    def lap_rows(src, first, last):
+        def one(i, carry):
+            laplace(src, first + lax.div(i, nby), lax.rem(i, nby))
+            return carry
+
+        lax.fori_loop(0, (last - first) * nby, one, 0)
+
+    def phase_sends(phase, src, sC, sK, rR, rC, rK, ready):
         copies = [None] * 8
-        for ex in order[:2]:
+        for s, ex in enumerate(order[:2]):
             ready(ex)
-            for ey in range(nby):
-                laplace(src, ex, ey)
-        for x in (0, nx - 1):
-            assemble_row(x)
-        if phase == 0:
-            pl.semaphore_wait(barrier, len(peers))
-        for s in range(2):
+            lap_rows(src, ex, ex + 1)
+            assemble_row(s * (nx - 1))
             for t in range(2):
-                k = 4 + 2 * s + t
-                copies[k] = send(
-                    phase, k, W.at[s * (nx - 1), t * (nq - 1)], rK.at[3 - 2 * s - t]
-                )
-        for s in range(2):
+                sK[2 * s + t] = corner(s, t)
+            if phase == 0 and s == 0:
+                pl.semaphore_wait(barrier, len(peers))
             copies[s] = send(phase, s, T.at[s * (nx - 1)], rR.at[1 - s])
+            for t in range(2):
+                k = 2 * s + t
+                copies[4 + k] = send(phase, 4 + k, sK.at[k], rK.at[3 - k])
         if phase == 0:
             for k in range(8):
                 masses.append(
                     pltpu.make_async_remote_copy(
-                        src_ref=mass_ref, dst_ref=rM.at[opposite[k]],
+                        src_ref=sM, dst_ref=rM.at[opposite[k]],
                         send_sem=mass_send.at[k], recv_sem=mass_recv.at[opposite[k]],
                         device_id=peers[k], device_id_type=MESH,
                     )
@@ -191,8 +212,7 @@
                 masses[-1].start()
         for ex in order[2:]:
             ready(ex)
-            for ey in range(nby):
-                laplace(src, ex, ey)
+        lap_rows(src, 1, nbx - 1)
         for k in range(nx // 2):
             a, b = rows_sum(2 * k, 0), rows_sum(2 * k + 1, 0)
             sC[0, k] = jnp.where(is_low, a, swap(b))
@@ -205,24 +225,35 @@
                 assemble_row(x)
         return copies
 
-    def finished(x, rR, rC, rK):
-        line = [T[x, q] for q in range(nq)]
-        if x in (0, nx - 1):
-            s = 0 if x == 0 else 1
-            line = [v + rR[s, q] for q, v in enumerate(line)]
-            line[0] = line[0] + low * swap(rK[2 * s])
-            line[-1] = line[-1] + high * swap(rK[2 * s + 1])
+    def finished(x, rR, rC, rK, out, done):
+        scale = lambda q, v: v * M[3, x, q]
+        for q in range(1, nq - 1):
+            if done(x, q):
+                continue
+            v = T[x, q]
+            if x in (0, nx - 1):
+                v = v + rR[0 if x == 0 else 1, q]
+            out[x, q] = scale(q, v)
+        ends = [T[x, 0], T[x, nq - 1]]
         before, after = rC[0, x // 2], rC[1, x // 2]
         if x % 2 == 0:
             after = swap(after)
         else:
             before = swap(before)
-        line[0] = line[0] + low * before
-        line[-1] = line[-1] + high * after
-        return line
+        ends = [ends[0] + low * before, ends[1] + high * after]
+        if x in (0, nx - 1):
+            s = 0 if x == 0 else 1
+            zero = jnp.zeros((nf, lanes), jnp.float32)
+            ends[0] = ends[0] + rR[s, 0] + jnp.concatenate([rK[2 * s], zero], axis=0)
+            ends[1] = ends[1] + rR[s, nq - 1] + jnp.concatenate([zero, rK[2 * s + 1]], axis=0)
+        out[x, 0] = scale(0, ends[0])
+        out[x, nq - 1] = scale(nq - 1, ends[1])
 
     masses = []
-    first_copies = phase_sends(0, raw, sC1, rR1, rC1, rK1, lambda ex: loads[ex].wait())
+
+    first_copies = phase_sends(
+        0, raw, sC1, sK1, rR1, rC1, rK1, lambda ex: loads[ex].wait()
+    )
 
     for copy in masses:
         copy.wait_recv()
@@ -231,37 +262,51 @@
     x_low, x_high = (x_at & 3) == 0, (x_at & 3) == 3
     y_low, y_high = (y_at & 3) == 0, (y_at & 3) == 3
 
-    def mass_rows(own, prev, nxt):
-        down = jnp.concatenate([prev[nx - 1:], own[: nx - 1]], axis=0)
-        up = jnp.concatenate([own[1:], nxt[:1]], axis=0)
-        return own + jnp.where(x_low, down, 0.0) + jnp.where(x_high, up, 0.0)
-
-    here = mass_rows(mass_ref[...], rM[0], rM[1])
-    left = mass_rows(rM[2], rM[4], rM[6])
-    right = mass_rows(rM[3], rM[5], rM[7])
-    back = jnp.concatenate([left[:, ny - 1:], here[:, : ny - 1]], axis=1)
-    ahead = jnp.concatenate([here[:, 1:], right[:, :1]], axis=1)
+    def edge_row(k, s):
+        return rM[k, pl.ds(s, 1), pl.ds(0, ny)]
+
+    def edge_column(k, t):
+        return jnp.sum(
+            jnp.where(diagonal, rM[k, pl.ds(2 + t, 1), pl.ds(0, nx)], 0.0), axis=1, keepdims=True
+        )
+
+    def mass_rows(own, prev, nxt, below, above):
+        down = jnp.concatenate([prev, own[: nx - 1]], axis=0)
+        up = jnp.concatenate([own[1:], nxt], axis=0)
+        return own + jnp.where(below, down, 0.0) + jnp.where(above, up, 0.0)
+
+    here = mass_rows(mass_ref[...], edge_row(0, 1), edge_row(1, 0), x_low, x_high)
+
+    def beside(k, t):
+        before = edge_row(4 + k, 1)[:, t * (ny - 1):t * (ny - 1) + 1]
+        after = edge_row(6 + k, 0)[:, t * (ny - 1):t * (ny - 1) + 1]
+        return mass_rows(edge_column(2 + k, t), before, after, x_low[:, :1], x_high[:, :1])
+
+    back = jnp.concatenate([beside(0, 1), here[:, : ny - 1]], axis=1)
+    ahead = jnp.concatenate([here[:, 1:], beside(1, 0)], axis=1)
     mass_sum = here + jnp.where(y_low, back, 0.0) + jnp.where(y_high, ahead, 0.0)
     split(3, 1.0 / mass_sum)
-    for x in range(nx):
+    def spread_mass(x, carry):
         spread_row(3, x)
+        return carry
+
+    lax.fori_loop(0, nx, spread_mass, 0)
 
     for copy in first_copies:
         copy.wait_recv()
     for x in range(nx):
-        line = finished(x, rR1, rC1, rK1)
-        for q in range(nq):
-            U[x, q] = line[q] * M[3, x, q]
+        finished(x, rR1, rC1, rK1, U, lambda x, q: False)
     for copy in first_copies:
         copy.wait_send()
 
-    second_copies = phase_sends(1, U, sC2, rR2, rC2, rK2, lambda ex: None)
+    second_copies = phase_sends(1, U, sC2, sK2, rR2, rC2, rK2, lambda ex: None)
+    for x in range(1, nx - 1):
+        for q in range(1, nq - 1):
+            out_ref[x, q] = T[x, q] * M[3, x, q]
     for copy in second_copies:
         copy.wait_recv()
     for x in range(nx):
-        line = finished(x, rR2, rC2, rK2)
-        for q in range(nq):
-            out_ref[x, q] = line[q] * M[3, x, q]
+        finished(x, rR2, rC2, rK2, out_ref, lambda x, q: 0 < x < nx - 1)
     for copy in second_copies + masses:
         copy.wait_send()
 
@@ -281,15 +326,16 @@
         def landing():
             return [
                 vmem(2, nx // 2, 2 * nf, lanes),
+                vmem(4, nf, lanes),
                 vmem(2, ny // 2, 2 * nf, lanes),
                 vmem(2, nx // 2, 2 * nf, lanes),
-                vmem(4, 2 * nf, lanes),
+                vmem(4, nf, lanes),
             ]
 
         out = pl.pallas_call(
             functools.partial(kernel, faces, cols, nf, nbx, nby),
             out_shape=jax.ShapeDtypeStruct(tiles, f32),
-            in_specs=[pl.BlockSpec(memory_space=pl.ANY)]
+            in_specs=[pl.BlockSpec(memory_space=pltpu.HBM)]
             + [pl.BlockSpec(memory_space=pltpu.VMEM)] * 3,
             out_specs=pl.BlockSpec(memory_space=pltpu.VMEM),
             scratch_shapes=[
@@ -299,7 +345,8 @@
                 vmem(*tiles),
                 vmem(*tiles),
                 vmem(4, nx, 3 * ny),
-                vmem(8, nx, ny),
+                vmem(4, 128),
+                vmem(8, 4, 128),
                 *landing(), *landing(),
                 pltpu.SemaphoreType.DMA((nbx,)),
                 pltpu.SemaphoreType.DMA((8,)),
@@ -308,11 +355,11 @@
                 pltpu.SemaphoreType.DMA((2, 8)),
             ],
             compiler_params=pltpu.CompilerParams(
-                collective_id=0, has_side_effects=True, vmem_limit_bytes=32 * 1024 * 1024
+                collective_id=0, has_side_effects=True, vmem_limit_bytes=66800000
             ),
         )(
             fields.transpose(1, 2, 0, 3).reshape(tiles),
-            metric_diag, metric_cross, point_mass,
+            metric_diag.transpose(1, 0, 2), metric_cross, point_mass,
         )
         return out.reshape(nx, ny, nf, lanes).transpose(2, 0, 1, 3)
 

time: 22 us -> 24.2 us (1.100)
  Pallas kernels: 18.8 us -> 21.7 us
  local copies, waits for them, and re-layouts: 2.79 us -> 2.09 us
    pallas_call x1, Pallas kernels: 18.8 us -> 21.7 us  [shards(): pl.pallas_call(functools.partial(kernel, faces, cols, nf, nbx, nby), out_...]
    unnamed x8 -> x1, local copies, waits for them, and re-layouts: 2.79 us -> 2.09 us
where the time goes in v3:
time: 24.2 us; the launch traced here: 23.8 us
  Pallas kernels  21.7 us (90%)
  local copies, waits for them, and re-layouts  2.09 us (9%)
    pallas_call x1, Pallas kernels, shards(): pl.pallas_call(functools.partial(kernel, faces, cols, nf, nbx, nby), out_...  21.7 us
    unnamed x1, local copies, waits for them, and re-layouts  2.09 us

profile of v3, /device:TPU:1, one launch (start us, length us, event | category | flops | bytes accessed | tf_op | source)
XLA Modules:
  0.0 23.8 jit_solution(6755894941956332919)
XLA Ops:
  0.0 21.7 %shard_map.46 = f32[20,10,8,128]{3,2,1,0:T(8,128)} custom-call(f32[20,10,8,128]{3,2,1,0:T(8,128)} %bitcast.8, f32[20,2,20]{2,1,0:T(2,128)} %bitcast.9, f32[20,20]{1,0:T(8,128)} %cross_ref.1, f32[20,20]{1,0:T(8,128)} %mass_ref.1), custom_call_target="tpu_custom_call" | custom-call | tf_op jit(solution)/shard_map/pallas_call | solution.py:335
  21.7 2.1 %copy.6 = f32[4,20,20,128]{3,0,2,1:T(4,128)} copy(f32[4,20,20,128]{3,0,2,1:T(4,128)} %bitcast.7) | data formatting | bytes 1638400
